TPU v7x, 32 devices: a whole 2x2x4 slice. The times are simulated.
32 devices in a mesh: groups: 2 (over x), strip: 16 (over z, y, core).
Axes of the slice: x: 2, y: 2, z: 4, core: 2. Of those that a mesh axis runs over, the one named last changes fastest.
Arguments:
- incoming_wave: float32 [8, 2, 256, 1024], P('groups', None, 'strip'), parts along dimension 0, may hold values from -64 to 64
- speed_class_map: int32 [4, 256, 1024], P('groups', 'strip'), parts along dimension 0, may hold values from 0 to 15
- spectral_entry_index: int32 [8, 4], P('groups'), parts along dimension 0, may hold values from 0 to 15
- filter_weights: float32 [16, 16, 2, 13], replicated, may hold values from -1.6 to 1.6
- scaled_pulsations: float32 [16], replicated, may hold values from 1 to 6
- inverse_speed_classes: float32 [16], replicated, may hold values from 0.3 to 1.5
Outputs:
- image: float32 [4, 256, 1024], P('groups', 'strip'), parts along dimension 0
- handed: float32 [8, 2, 256, 1024], P('groups', None, 'strip'), parts along dimension 0
There are 2 independent parts, one for each index of `groups`. A program takes and returns all parts, laid end to end along the dimension named above; an argument that names none is the same for every part. Nothing has to cross between parts.
All inputs are finite; a program needn't handle non-finite values.
Results may differ from a plain program's by a relative error of at most 0.0003.
Values sent between devices are 32-bit elements; how exact they have to be, the bound alone decides.
A program may use at most 128 MiB of HBM per device.

v0:
```python
import functools
import jax
import jax.numpy as jnp
from jax import lax
from jax.experimental import pallas as pl
from jax.experimental.pallas import tpu as pltpu
from jax.sharding import PartitionSpec as P

SECTIONS = 4
LEVELS = 2
ORDER = 12
NFREQ = 4
NBIN = 16
NW = 16


def extended_2(shard, sides, width):
    for axis, dim in sides:
        devices, length = (lax.axis_size(axis), shard.shape[dim])
        up = [(i, (i + 1) % devices) for i in range(devices)]
        down = [(j, i) for i, j in up]
        last = lax.slice_in_dim(shard, length - width, length, axis=dim)
        initial = lax.slice_in_dim(shard, 0, width, axis=dim)
        before = lax.ppermute(last, axis, up)
        after = lax.ppermute(initial, axis, down)
        shard = jnp.concatenate([before, shard, after], axis=dim)
    return shard


def from_behind(shard, axis, by):
    devices = lax.axis_size(axis)
    return lax.ppermute(shard, axis, [(i, (i + by) % devices) for i in range(devices)])


def stencil_padded(padded):
    vertical = padded[:, :, :-2, :] + padded[:, :, 2:, :]
    middle = padded[:, :, 1:-1, :]
    return (
        -0.5 * middle[..., 1:-1]
        + 0.25 * (vertical[..., 1:-1] + middle[..., :-2] + middle[..., 2:])
        + 0.125 * (vertical[..., :-2] + vertical[..., 2:])
    )


def complex_times(coeff, field):
    real_part = coeff[:, 0] * field[:, 0] - coeff[:, 1] * field[:, 1]
    imag_part = coeff[:, 0] * field[:, 1] + coeff[:, 1] * field[:, 0]
    return jnp.stack([real_part, imag_part], axis=1)


def shards(
    incoming_wave,
    speed_class_map,
    spectral_entry_index,
    filter_weights,
    scaled_pulsations,
    inverse_speed_classes,
):
    highest = lax.Precision.HIGHEST
    summed_along = incoming_wave.shape[2]
    summed_across = incoming_wave.shape[3]
    strip_count = lax.axis_size("strip")
    lateral_count = strip_count // SECTIONS
    position = (lax.axis_index("strip") - lateral_count // 2) % strip_count
    vertical_slab = position // lateral_count
    lateral_place = position % lateral_count
    section_rows = summed_along * lateral_count
    section_cells = section_rows * summed_across
    margin = ORDER
    extended_rows = summed_along + 2 * margin
    lateral_rows = (
        lateral_place * summed_along - margin + jnp.arange(extended_rows, dtype=jnp.int32)
    )
    inside = ((lateral_rows >= 0) & (lateral_rows < section_rows)).astype(jnp.float32)[
        None, None, :, None
    ]

    def mcclellan_step(field):
        padded = jnp.pad(field, ((0, 0), (0, 0), (1, 1), (0, 0)))
        padded = jnp.pad(padded, ((0, 0), (0, 0), (0, 0), (1, 1)))
        result = stencil_padded(padded)
        result = result * inside
        return result

    def interior(field):
        return field[:, :, margin : margin + summed_along, :]

    def image_downward(field, batch_index):
        freq_row = lax.dynamic_index_in_dim(spectral_entry_index, batch_index, 0, keepdims=False)
        freq_select = (freq_row[:, None] == jnp.arange(NW, dtype=jnp.int32)[None, :]).astype(
            jnp.float32
        )
        freq_coeffs = jnp.einsum("fw,wbck->fbck", freq_select, filter_weights, precision=highest)
        freq_omega = jnp.dot(freq_select, scaled_pulsations, precision=highest)
        wavefield = field
        raws = []
        for level in range(LEVELS):
            cells = speed_class_map[level].reshape(-1)
            bin_onehot = (cells[None, :] == jnp.arange(NBIN, dtype=jnp.int32)[:, None]).astype(
                jnp.float32
            )
            cell_slowness = jnp.dot(inverse_speed_classes, bin_onehot, precision=highest).reshape(
                summed_along, summed_across
            )
            table = jnp.einsum("fbck,bn->kfcn", freq_coeffs, bin_onehot, precision=highest).reshape(
                ORDER + 1, NFREQ, 2, summed_along, summed_across
            )
            extended = extended_2(wavefield, (("strip", 2),), ORDER) * inside
            previous = extended
            current = mcclellan_step(extended)
            accumulated = complex_times(table[0], interior(previous)) + complex_times(
                table[1], interior(current)
            )

            def recursion_step(order_index, state_tuple):
                before, present, running = state_tuple
                following = 2.0 * mcclellan_step(present) - before
                coeff = lax.dynamic_index_in_dim(table, order_index, 0, keepdims=False)
                running = running + complex_times(coeff, interior(following))
                return (present, following, running)

            previous, current, accumulated = lax.fori_loop(
                2, ORDER + 1, recursion_step, (previous, current, accumulated)
            )
            phase_angle = freq_omega[:, None, None] * cell_slowness[None]
            cosine = jnp.cos(phase_angle)
            sine_part = jnp.sin(phase_angle)
            real_part = accumulated[:, 0] * cosine - accumulated[:, 1] * sine_part
            imag_part = accumulated[:, 0] * sine_part + accumulated[:, 1] * cosine
            wavefield = jnp.stack([real_part, imag_part], axis=1)
            raws.append(jnp.sum(real_part, axis=0))
        return (wavefield, raws)

    above_floor_lines, above_unscaled_waves = image_downward(incoming_wave, vertical_slab)
    arriving = from_behind(above_floor_lines, "strip", lateral_count)
    second_bottom, second_raws = image_downward(arriving, jnp.maximum(vertical_slab - 1, 0))
    handed = jnp.where(vertical_slab == 0, above_floor_lines, second_bottom)
    first_section = (vertical_slab > 0).astype(jnp.float32)
    totals = [
        above_unscaled_waves[level] + first_section * second_raws[level] for level in range(LEVELS)
    ]
    selector = (jnp.arange(SECTIONS, dtype=jnp.int32) == vertical_slab).astype(jnp.float32)
    images = []
    for level in range(LEVELS):
        raw_image = totals[level]
        spread = lax.psum(selector * jnp.sum(raw_image * raw_image), "strip")
        mean_square = jnp.sum(spread * selector) / section_cells
        images.append(raw_image / jnp.sqrt(mean_square + 1e-06))
    return (jnp.stack(images, axis=0), handed)


SUB = 8
LANES = 128
PAD = 1
UNROLL = 4
MESH = pl.DeviceIdType.MESH


def at_row(row):
    return pl.ds(pl.multiple_of(row * SUB, SUB), SUB)


def kernel(
    strip_count,
    entry_ref,
    wave_ref,
    map_ref,
    table_ref,
    image_ref,
    handed_ref,
    starts,
    work,
    bottom,
    last,
    last_in,
    wave_out,
    map_out,
    map_all,
    raw,
    raw_in,
    sum_own,
    sum_in,
    swap_sems,
    halo_sems,
    hand_sems,
    fin_sems,
    raw_sems,
    sum_sems,
):
    nfh = wave_ref.shape[0] // 2
    length = wave_ref.shape[2]
    rows = 2 * length
    blocks = wave_ref.shape[3] // LANES
    lateral = strip_count // SECTIONS
    shift = lateral // 2
    pairs = lateral // 2
    margin = ORDER
    first = PAD + margin
    me = lax.axis_index("strip")
    position = lax.rem(me + strip_count - shift, strip_count)
    section = position // lateral
    place = lax.rem(position, lateral)
    pair = place // 2
    half = lax.rem(place, 2)
    up = jnp.where(pair > 0, 1, 0)
    down = jnp.where(pair < pairs - 1, 1, 0)
    has_up = pair > 0
    has_down = pair < pairs - 1
    has_before = section > 0
    has_after = section < SECTIONS - 1
    other = 1 - half

    def device(pos):
        return {"strip": lax.rem(pos + shift + strip_count, strip_count)}

    partner = device(position + 1 - 2 * half)
    upper = device(position - 2)
    lower = device(position + 2)
    deeper = device(position + lateral)
    shallower = device(position + strip_count - lateral)

    def remote(src, dst, sems, index, target):
        return pltpu.make_async_remote_copy(
            src_ref=src,
            dst_ref=dst,
            send_sem=sems.at[(0,) + index],
            recv_sem=sems.at[(1,) + index],
            device_id=target,
            device_id_type=MESH,
        )

    def span(row, count):
        return pl.ds(pl.multiple_of(row * SUB, SUB), count * SUB)

    zero = jnp.zeros((SUB, LANES), jnp.float32)
    for edge in (first - 1, first + rows):
        for f in range(nfh):
            for c in range(2):
                for s in range(2 * LEVELS):
                    starts[s, f, c, at_row(edge), :] = zero
        for c in range(2):
            for k in range(ORDER):
                work[k, c, at_row(edge), :] = zero

    barrier = pltpu.get_barrier_semaphore()
    for d in range(1, lateral):
        mate = device(section * lateral + lax.rem(place + d, lateral))
        pl.semaphore_signal(barrier, inc=1, device_id=mate, device_id_type=MESH)
    for target in (deeper, shallower):
        pl.semaphore_signal(barrier, inc=1, device_id=target, device_id_type=MESH)

    def rearrange(load, store):
        for g in range(length // SUB):
            for j in range(blocks):
                store(g, j, load(g, j))

    def strided(row, g, j):
        return pl.ds((row + g * SUB) * SUB + j, SUB, stride=SUB)

    own_row = half * length
    for f in range(nfh):
        for c in range(2):
            rearrange(
                lambda g, j: wave_ref[other * nfh + f, c, pl.ds(g * SUB, SUB), pl.ds(j * LANES, LANES)],
                lambda g, j, x: pltpu_store(wave_out.at[f, c], strided(0, g, j), x),
            )
    for l in range(LEVELS):
        rearrange(
            lambda g, j: map_ref[l, pl.ds(g * SUB, SUB), pl.ds(j * LANES, LANES)],
            lambda g, j, x: pltpu_store(map_out.at[l], strided(0, g, j), x),
        )
    pl.semaphore_wait(barrier, lateral + 1)
    swaps = []
    for f in range(nfh):
        copy = remote(
            wave_out.at[f],
            starts.at[0, f, :, span(first + own_row, length), :],
            swap_sems,
            (f,),
            partner,
        )
        copy.start()
        swaps.append(copy)
    copy = remote(
        map_out, map_all.at[:, span(own_row, length), :], swap_sems, (nfh,), partner
    )
    copy.start()
    swaps.append(copy)
    for f in range(nfh):
        for c in range(2):
            rearrange(
                lambda g, j: wave_ref[half * nfh + f, c, pl.ds(g * SUB, SUB), pl.ds(j * LANES, LANES)],
                lambda g, j, x: pltpu_store(
                    starts.at[0, f, c], strided(first + own_row, g, j), x
                ),
            )
    for l in range(LEVELS):
        rearrange(
            lambda g, j: map_ref[l, pl.ds(g * SUB, SUB), pl.ds(j * LANES, LANES)],
            lambda g, j, x: pltpu_store(map_all.at[l], strided(own_row, g, j), x),
        )

    def halo_up(stage, f):
        ref = starts.at[stage, f]
        return remote(
            ref.at[:, span(first, margin), :],
            ref.at[:, span(first + rows, margin), :],
            halo_sems,
            (stage, f, 0),
            upper,
        )

    def halo_down(stage, f):
        ref = starts.at[stage, f]
        return remote(
            ref.at[:, span(first + rows - margin, margin), :],
            ref.at[:, span(first - margin, margin), :],
            halo_sems,
            (stage, f, 1),
            lower,
        )

    def send_halo(stage, f):
        pl.when(has_up)(lambda: halo_up(stage, f).start())
        pl.when(has_down)(lambda: halo_down(stage, f).start())

    def wait_halo(stage, f):
        pl.when(has_down)(lambda: halo_up(stage, f).wait_recv())
        pl.when(has_up)(lambda: halo_down(stage, f).wait_recv())

    def hand_parts(f):
        parts = ((0, margin), (rows - margin, margin), (margin, rows - 2 * margin))
        return [
            remote(
                bottom.at[f, :, span(row, count), :],
                starts.at[LEVELS, f, :, span(first + row, count), :],
                hand_sems,
                (f, n),
                deeper,
            )
            for n, (row, count) in enumerate(parts)
        ]

    lane = lax.broadcasted_iota(jnp.int32, (SUB, LANES), 1)
    sub = lax.broadcasted_iota(jnp.int32, (SUB, LANES), 0)
    at_first = lane == 0
    at_last = lane == LANES - 1
    keep_first = sub > 0
    keep_last = sub < SUB - 1

    def across(u):
        right = pltpu.roll(u, 1, 1)
        right_fix = jnp.where(keep_first, pltpu.roll(right, 1, 0), 0.0)
        left = pltpu.roll(u, LANES - 1, 1)
        left_fix = jnp.where(keep_last, pltpu.roll(left, SUB - 1, 0), 0.0)
        return jnp.where(at_first, right_fix, right) + jnp.where(at_last, left_fix, left)

    def reach(k):
        return ((margin - k + UNROLL - 1) // UNROLL) * UNROLL

    def apply(k, present, before, target):
        extra = reach(k)
        low = first - up * extra
        count = (rows + (up + down) * extra) // UNROLL

        def block(i, carry):
            base = low + i * UNROLL
            for c in range(2):
                v = [present[c, at_row(base - 1 + n), :] for n in range(UNROLL + 2)]
                q = [v[n] + v[n + 1] for n in range(UNROLL + 1)]
                for n in range(UNROLL):
                    u = q[n] + q[n + 1]
                    w = across(u) + (u + u)
                    centre = v[n + 1]
                    if before is None:
                        value = 0.125 * w - centre
                    else:
                        old = before[c, at_row(base + n), :]
                        value = 0.25 * w - (centre + centre + old)
                    target[c, at_row(base + n), :] = value
            return carry

        lax.fori_loop(0, count, block, 0)

    def unit(tick, level, f):
        stage = tick * LEVELS + level
        start = starts.at[stage, f]
        apply(1, start, None, work.at[0])
        apply(2, work.at[0], start, work.at[1])

        def step(k, carry):
            apply(k, work.at[k - 2], work.at[k - 3], work.at[k - 1])
            return carry

        lax.fori_loop(3, ORDER + 1, step, 0)
        batch = section if tick == 0 else jnp.maximum(section - 1, 0)
        entry = entry_ref[batch, half * nfh + f]

        def combine(i, carry):
            spots = [2 * i, 2 * i + 1]
            bins = [map_all[level, at_row(r), :] for r in spots]
            real = [None] * 2
            imag = [None] * 2
            for k in range(ORDER + 1):
                rows_of = [
                    jnp.broadcast_to(table_ref[entry, pl.ds(2 * k + c, 1), :], (SUB, LANES))
                    for c in range(2)
                ]
                source = start if k == 0 else work.at[k - 1]
                for n, r in enumerate(spots):
                    cr, ci = (
                        jnp.take_along_axis(t, bins[n], axis=1, mode="promise_in_bounds")
                        for t in rows_of
                    )
                    tr = source[0, at_row(first + r), :]
                    ti = source[1, at_row(first + r), :]
                    re = cr * tr - ci * ti
                    im = cr * ti + ci * tr
                    real[n] = re if k == 0 else real[n] + re
                    imag[n] = im if k == 0 else imag[n] + im
            for n, r in enumerate(spots):
                re, im = real[n], imag[n]
                if tick == 0 and f == 0:
                    raw[level, at_row(r), :] = re
                else:
                    part = re if tick == 0 else jnp.where(has_before, re, 0.0)
                    raw[level, at_row(r), :] = raw[level, at_row(r), :] + part
                for c, value in enumerate((re, im)):
                    if level < LEVELS - 1:
                        starts[stage + 1, f, c, at_row(first + r), :] = value
                    elif tick == 0:
                        bottom[f, c, at_row(r), :] = value
                    else:
                        last[f, c, at_row(r), :] = jnp.where(
                            has_before, value, bottom[f, c, at_row(r), :]
                        )
            return carry

        lax.fori_loop(0, rows // 2, combine, 0)

    def finish_wave(f):
        return remote(
            last.at[f, :, span(other * length, length), :],
            last_in.at[f],
            fin_sems,
            (f,),
            partner,
        )

    def finish_raw(l):
        return remote(
            raw.at[l, span(other * length, length), :], raw_in.at[l], raw_sems, (l,), partner
        )

    for f in range(nfh):
        swaps[f].wait_recv()
        send_halo(0, f)
    swaps[nfh].wait_recv()
    for level in range(LEVELS):
        for f in range(nfh):
            wait_halo(level, f)
            unit(0, level, f)
            if level < LEVELS - 1:
                send_halo(level + 1, f)
            else:

                @pl.when(has_after)
                def _():
                    for copy in hand_parts(f):
                        copy.start()

    def forward(f):
        @pl.when(has_before)
        def _():
            for copy in hand_parts(f):
                copy.wait_recv()

            send_halo(LEVELS, f)

    def skip_or(fn):
        pl.when(has_before)(fn)

    for f in range(nfh):
        forward(f)
    for level in range(LEVELS):
        for f in range(nfh):

            @pl.when(has_before)
            def _():
                wait_halo(LEVELS + level, f)

            unit(1, level, f)
            if level < LEVELS - 1:

                @pl.when(has_before)
                def _():
                    send_halo(LEVELS + level + 1, f)

            else:
                finish_wave(f).start()
        finish_raw(level).start()

    for l in range(LEVELS):
        finish_raw(l).wait_recv()

        def merge(i, carry):
            value = raw[l, at_row(own_row + i), :] + raw_in[l, at_row(i), :]
            raw_in[l, at_row(i), :] = value
            return carry + value * value

        sum_own[pl.ds(l * SUB, SUB), :] = lax.fori_loop(0, length, merge, zero)
    for d in range(1, lateral):
        mate = device(section * lateral + lax.rem(place + d, lateral))
        remote(sum_own, sum_in.at[d], sum_sems, (d,), mate).start()

    for f in range(nfh):
        for c in range(2):
            rearrange(
                lambda g, j: last[f, c, strided(own_row, g, j), :],
                lambda g, j, x: out_store(handed_ref, half * nfh + f, c, g, j, x),
            )
    for f in range(nfh):
        finish_wave(f).wait_recv()
        for c in range(2):
            rearrange(
                lambda g, j: last_in[f, c, strided(0, g, j), :],
                lambda g, j, x: out_store(handed_ref, other * nfh + f, c, g, j, x),
            )

    total = sum_own[...]
    for d in range(1, lateral):
        mate = device(section * lateral + lax.rem(place + d, lateral))
        remote(sum_own, sum_in.at[d], sum_sems, (d,), mate).wait_recv()
        total = total + sum_in[d]
    cells = length * lateral * blocks * LANES
    for l in range(LEVELS):
        mean = jnp.sum(total[l * SUB : (l + 1) * SUB], axis=(0, 1), keepdims=True) / cells
        scale = jnp.broadcast_to(1.0 / jnp.sqrt(mean + 1e-06), (SUB, LANES))

        def put(g, j, x):
            image_ref[l, pl.ds(g * SUB, SUB), pl.ds(j * LANES, LANES)] = x * scale

        rearrange(lambda g, j: raw_in[l, strided(0, g, j), :], put)

    for copy in swaps:
        copy.wait_send()
    for f in range(nfh):
        send_done = lambda make, stage: make(stage, f).wait_send()
        for stage in range(2 * LEVELS):
            live_up = has_up if stage < LEVELS else has_up & has_before
            live_down = has_down if stage < LEVELS else has_down & has_before
            pl.when(live_up)(lambda: send_done(halo_up, stage))
            pl.when(live_down)(lambda: send_done(halo_down, stage))

        @pl.when(has_after)
        def _():
            for copy in hand_parts(f):
                copy.wait_send()

        finish_wave(f).wait_send()
    for l in range(LEVELS):
        finish_raw(l).wait_send()
    for d in range(1, lateral):
        mate = device(section * lateral + lax.rem(place + d, lateral))
        remote(sum_own, sum_in.at[d], sum_sems, (d,), mate).wait_send()


def pltpu_store(ref, where, x):
    ref[where, :] = x


def out_store(ref, f, c, g, j, x):
    ref[f, c, pl.ds(g * SUB, SUB), pl.ds(j * LANES, LANES)] = x


def paired(
    incoming_wave,
    speed_class_map,
    spectral_entry_index,
    filter_weights,
    scaled_pulsations,
    inverse_speed_classes,
):
    strip_count = lax.axis_size("strip")
    lateral = strip_count // SECTIONS
    length = incoming_wave.shape[2]
    nfh = NFREQ // 2
    rows = 2 * length
    tall = (rows + 2 * ORDER + 2 * PAD) * SUB
    angle = scaled_pulsations[:, None] * inverse_speed_classes[None, :]
    cosine = jnp.cos(angle)[:, None, :]
    sine = jnp.sin(angle)[:, None, :]
    by_order = jnp.transpose(filter_weights, (2, 0, 3, 1))
    real = by_order[0] * cosine - by_order[1] * sine
    imag = by_order[0] * sine + by_order[1] * cosine
    table = jnp.stack([real, imag], axis=2).reshape(NW, 2 * (ORDER + 1), NBIN)
    table = jnp.pad(table, ((0, 0), (0, 0), (0, LANES - NBIN)))
    f32 = jnp.float32
    vmem = pl.BlockSpec(memory_space=pltpu.VMEM)

    def dma(*shape):
        return pltpu.SemaphoreType.DMA((2,) + shape)

    return pl.pallas_call(
        functools.partial(kernel, strip_count),
        out_shape=(
            jax.ShapeDtypeStruct(speed_class_map.shape, f32),
            jax.ShapeDtypeStruct(incoming_wave.shape, f32),
        ),
        in_specs=[pl.BlockSpec(memory_space=pltpu.SMEM), vmem, vmem, vmem],
        out_specs=(vmem, vmem),
        scratch_shapes=[
            pltpu.VMEM((2 * LEVELS, nfh, 2, tall, LANES), f32),
            pltpu.VMEM((ORDER, 2, tall, LANES), f32),
            pltpu.VMEM((nfh, 2, rows * SUB, LANES), f32),
            pltpu.VMEM((nfh, 2, rows * SUB, LANES), f32),
            pltpu.VMEM((nfh, 2, length * SUB, LANES), f32),
            pltpu.VMEM((nfh, 2, length * SUB, LANES), f32),
            pltpu.VMEM((LEVELS, length * SUB, LANES), jnp.int32),
            pltpu.VMEM((LEVELS, rows * SUB, LANES), jnp.int32),
            pltpu.VMEM((LEVELS, rows * SUB, LANES), f32),
            pltpu.VMEM((LEVELS, length * SUB, LANES), f32),
            pltpu.VMEM((LEVELS * SUB, LANES), f32),
            pltpu.VMEM((lateral, LEVELS * SUB, LANES), f32),
            dma(nfh + 1),
            dma(2 * LEVELS, nfh, 2),
            dma(nfh, 3),
            dma(nfh),
            dma(LEVELS),
            dma(lateral),
        ],
        compiler_params=pltpu.CompilerParams(
            collective_id=0, has_side_effects=True, vmem_limit_bytes=48 * 1024 * 1024
        ),
    )(spectral_entry_index, incoming_wave, speed_class_map, table)


def fits(mesh):
    lateral = mesh.shape["strip"] // SECTIONS
    return NFREQ % 2 == 0 and lateral % 4 == 0


def body_for(mesh):
    def body(wave, *rest):
        whole = wave.shape[3] == SUB * LANES and wave.shape[2] % SUB == 0
        if fits(mesh) and whole and wave.shape[2] >= ORDER:
            return paired(wave, *rest)
        return shards(wave, *rest)

    return body


def solution(mesh):
    return jax.shard_map(
        body_for(mesh),
        mesh=mesh,
        in_specs=(
            P("groups", None, "strip", None),
            P("groups", "strip", None),
            P("groups", None),
            P(),
            P(),
            P(),
        ),
        out_specs=(P("groups", "strip", None), P("groups", None, "strip", None)),
        check_vma=False,
    )
```

profile of v0, /device:TPU:0, one launch (start us, length us, event | category | flops | bytes accessed | tf_op | source)
XLA Modules:
  0.0 217.2 jit_solution(3326696068576645150)
XLA Ops:
  0.6 0.0 copy-start.3
  0.6 0.0 copy-start.4
  0.6 0.6 copy-done.3
  1.3 0.0 copy-done.4
  1.3 0.1 multiply_cosine_fusion
  1.4 1.3 multiply_subtract_fusion
  2.7 0.2 pad_maximum_fusion
  3.0 0.0 copy-start
  3.0 0.1 copy.9
  3.1 0.0 copy-start.1
  3.1 0.0 copy-start.2
  3.1 0.9 copy-done
  4.0 0.0 copy-done.1
  4.1 0.0 copy-done.2
  4.1 211.7 %shard_map.77 = (f32[2,16,1024]{2,1,0:T(8,128)S(1)}, f32[4,2,16,1024]{3,2,1,0:T(8,128)S(1)}) custom-call(s32[4,4]{1,0:T(4,128)S(1)} %copy-done.2, f32[4,2,16,1024]{3,2,1,0:T(8,128)S(1)} %copy-done, s32[2,16,1024]{2,1,0:T(8,128)S(1)} %copy-done.1, f32[16,26,128]{2,1,0:T(8,128)S(1)} %pad.4.table_ref), custom_call_target="tpu_custom_call" | custom-call | tf_op jit(solution)/shard_map/pallas_call | solution.py:604
  215.8 0.7 copy.12
  216.5 0.8 copy.13
  (2 shorter events, 0.0 us)
Async XLA Ops:
  0.6 0.7 copy-start.3
  0.6 0.7 copy-start.4
  3.0 1.0 copy-start
  3.1 1.0 copy-start.1
  3.1 1.0 copy-start.2
where the time goes:
time: 218 us; the launch traced here: 217 us
  Pallas kernels  212 us (97%)
  local copies, waits for them, and re-layouts  3.17 us (1%)
    pallas_call x1, Pallas kernels, paired(): pl.pallas_call(functools.partial(kernel, strip_count), out_shape=(jax.Sha...  212 us

commit v1 on v0

--- a/solution.py
+++ b/solution.py
@@ -151,8 +151,9 @@
 
 SUB = 8
 LANES = 128
-PAD = 1
-UNROLL = 4
+PAD = 5
+UNROLL = 8
+TOGETHER = 4
 MESH = pl.DeviceIdType.MESH
 
 
@@ -258,20 +259,15 @@
         return pl.ds((row + g * SUB) * SUB + j, SUB, stride=SUB)
 
     own_row = half * length
+    swaps = []
     for f in range(nfh):
         for c in range(2):
             rearrange(
                 lambda g, j: wave_ref[other * nfh + f, c, pl.ds(g * SUB, SUB), pl.ds(j * LANES, LANES)],
                 lambda g, j, x: pltpu_store(wave_out.at[f, c], strided(0, g, j), x),
             )
-    for l in range(LEVELS):
-        rearrange(
-            lambda g, j: map_ref[l, pl.ds(g * SUB, SUB), pl.ds(j * LANES, LANES)],
-            lambda g, j, x: pltpu_store(map_out.at[l], strided(0, g, j), x),
-        )
-    pl.semaphore_wait(barrier, lateral + 1)
-    swaps = []
-    for f in range(nfh):
+        if f == 0:
+            pl.semaphore_wait(barrier, lateral + 1)
         copy = remote(
             wave_out.at[f],
             starts.at[0, f, :, span(first + own_row, length), :],
@@ -281,6 +277,11 @@
         )
         copy.start()
         swaps.append(copy)
+    for l in range(LEVELS):
+        rearrange(
+            lambda g, j: map_ref[l, pl.ds(g * SUB, SUB), pl.ds(j * LANES, LANES)],
+            lambda g, j, x: pltpu_store(map_out.at[l], strided(0, g, j), x),
+        )
     copy = remote(
         map_out, map_all.at[:, span(own_row, length), :], swap_sems, (nfh,), partner
     )
@@ -365,24 +366,35 @@
 
         def block(i, carry):
             base = low + i * UNROLL
+            v = [
+                [present[c, at_row(base - 1 + n), :] for n in range(UNROLL + 2)]
+                for c in range(2)
+            ]
+            old = None
+            if before is not None:
+                old = [
+                    [before[c, at_row(base + n), :] for n in range(UNROLL)] for c in range(2)
+                ]
+            values = []
             for c in range(2):
-                v = [present[c, at_row(base - 1 + n), :] for n in range(UNROLL + 2)]
-                q = [v[n] + v[n + 1] for n in range(UNROLL + 1)]
+                q = [v[c][n] + v[c][n + 1] for n in range(UNROLL + 1)]
                 for n in range(UNROLL):
                     u = q[n] + q[n + 1]
                     w = across(u) + (u + u)
-                    centre = v[n + 1]
-                    if before is None:
+                    centre = v[c][n + 1]
+                    if old is None:
                         value = 0.125 * w - centre
                     else:
-                        old = before[c, at_row(base + n), :]
-                        value = 0.25 * w - (centre + centre + old)
-                    target[c, at_row(base + n), :] = value
+                        value = 0.25 * w - (centre + centre + old[c][n])
+                    values.append(value)
+            for c in range(2):
+                for n in range(UNROLL):
+                    target[c, at_row(base + n), :] = values[c * UNROLL + n]
             return carry
 
         lax.fori_loop(0, count, block, 0)
 
-    def unit(tick, level, f):
+    def unit(tick, level, f, meanwhile=None):
         stage = tick * LEVELS + level
         start = starts.at[stage, f]
         apply(1, start, None, work.at[0])
@@ -393,25 +405,30 @@
             return carry
 
         lax.fori_loop(3, ORDER + 1, step, 0)
+        if meanwhile is not None:
+            meanwhile()
         batch = section if tick == 0 else jnp.maximum(section - 1, 0)
         entry = entry_ref[batch, half * nfh + f]
 
         def combine(i, carry):
-            spots = [2 * i, 2 * i + 1]
+            spots = [TOGETHER * i + n for n in range(TOGETHER)]
             bins = [map_all[level, at_row(r), :] for r in spots]
-            real = [None] * 2
-            imag = [None] * 2
-            for k in range(ORDER + 1):
-                rows_of = [
-                    jnp.broadcast_to(table_ref[entry, pl.ds(2 * k + c, 1), :], (SUB, LANES))
-                    for c in range(2)
-                ]
-                source = start if k == 0 else work.at[k - 1]
-                for n, r in enumerate(spots):
+            real = [None] * TOGETHER
+            imag = [None] * TOGETHER
+            for n, r in enumerate(spots):
+                for k in range(ORDER + 1):
                     cr, ci = (
-                        jnp.take_along_axis(t, bins[n], axis=1, mode="promise_in_bounds")
-                        for t in rows_of
+                        jnp.take_along_axis(
+                            jnp.broadcast_to(
+                                table_ref[entry, pl.ds(2 * k + c, 1), :], (SUB, LANES)
+                            ),
+                            bins[n],
+                            axis=1,
+                            mode="promise_in_bounds",
+                        )
+                        for c in range(2)
                     )
+                    source = start if k == 0 else work.at[k - 1]
                     tr = source[0, at_row(first + r), :]
                     ti = source[1, at_row(first + r), :]
                     re = cr * tr - ci * ti
@@ -436,7 +453,7 @@
                         )
             return carry
 
-        lax.fori_loop(0, rows // 2, combine, 0)
+        lax.fori_loop(0, rows // TOGETHER, combine, 0)
 
     def finish_wave(f):
         return remote(
@@ -472,16 +489,17 @@
     def forward(f):
         @pl.when(has_before)
         def _():
-            for copy in hand_parts(f):
-                copy.wait_recv()
-
-            send_halo(LEVELS, f)
+            high, low, mid = hand_parts(f)
+            high.wait_recv()
+            pl.when(has_up)(lambda: halo_up(LEVELS, f).start())
+            low.wait_recv()
+            pl.when(has_down)(lambda: halo_down(LEVELS, f).start())
+            mid.wait_recv()
 
     def skip_or(fn):
         pl.when(has_before)(fn)
 
-    for f in range(nfh):
-        forward(f)
+    forward(0)
     for level in range(LEVELS):
         for f in range(nfh):
 
@@ -489,7 +507,8 @@
             def _():
                 wait_halo(LEVELS + level, f)
 
-            unit(1, level, f)
+            later = f + 1 if level == 0 and f + 1 < nfh else None
+            unit(1, level, f, None if later is None else lambda: forward(later))
             if level < LEVELS - 1:
 
                 @pl.when(has_before)

time: 218 us -> 102 us (0.47)
  Pallas kernels: 212 us -> 96.6 us
    pallas_call x1, Pallas kernels: 212 us -> 96.6 us  [paired(): pl.pallas_call(functools.partial(kernel, strip_count), out_shape=(jax.Sha...]
where the time goes in v1:
time: 102 us
  Pallas kernels  96.6 us (95%)
  local copies, waits for them, and re-layouts  3.17 us (3%)
  other arithmetic  1.64 us (2%)
    pallas_call x1, Pallas kernels, paired(): pl.pallas_call(functools.partial(kernel, strip_count), out_shape=(jax.Sha...  96.6 us
    unnamed x12, local copies, waits for them, and re-layouts  3.06 us

profile of v1, /device:TPU:0, one launch (start us, length us, event | category | flops | bytes accessed | tf_op | source)
XLA Modules:
  0.0 102.1 jit_solution(17472569692255793161)
XLA Ops:
  0.6 0.0 copy-start.3
  0.6 0.0 copy-start.4
  0.6 0.6 copy-done.3
  1.3 0.0 copy-done.4
  1.3 0.1 multiply_cosine_fusion
  1.4 1.3 %multiply_subtract_fusion = (f32[16,13,1,16]{3,2,1,0:T(1,128)S(1)}, f32[16,13,1,16]{3,2,1,0:T(1,128)S(1)}) fusion(f32[2,16,13,16]{3,0,2,1:T(2,128)} %bitcast.15, f32[16,16]{1,0:T(8,128)S(1)} %get-tuple-element.5, f32[16,16]{1,0:T(8,128)S(1)} %get-tuple-element.4), kind=kLoop, calls=%fused_computation.4 | loop fusion | flops 19968 | bytes 55296 | tf_op jit(solution)/shard_map/sub | solution.py:613
  2.7 0.2 pad_maximum_fusion
  3.0 0.0 copy-start
  3.0 0.1 copy.9
  3.1 0.0 copy-start.1
  3.1 0.0 copy-start.2
  3.1 0.9 copy-done
  4.0 0.0 copy-done.1
  4.1 0.0 copy-done.2
  4.1 96.6 %shard_map.77 = (f32[2,16,1024]{2,1,0:T(8,128)S(1)}, f32[4,2,16,1024]{3,2,1,0:T(8,128)S(1)}) custom-call(s32[4,4]{1,0:T(4,128)S(1)} %copy-done.2, f32[4,2,16,1024]{3,2,1,0:T(8,128)S(1)} %copy-done, s32[2,16,1024]{2,1,0:T(8,128)S(1)} %copy-done.1, f32[16,26,128]{2,1,0:T(8,128)S(1)} %pad.4.table_ref), custom_call_target="tpu_custom_call" | custom-call | tf_op jit(solution)/shard_map/pallas_call | solution.py:623
  100.6 0.7 copy.12
  101.3 0.8 copy.13
  (2 shorter events, 0.0 us)
Async XLA Ops:
  0.6 0.7 copy-start.3
  0.6 0.7 copy-start.4
  3.0 1.0 %copy-start = (f32[4,2,16,1024]{3,2,1,0:T(8,128)S(1)}, f32[4,2,16,1024]{3,2,1,0:T(8,128)}, u32[]{:S(2)}) copy-start(f32[4,2,16,1024]{3,2,1,0:T(8,128)} %wave_ref.1) | copy-start | bytes 1572868
  3.1 1.0 copy-start.1
  3.1 1.0 copy-start.2
